TPU v7x, 32 devices: a whole 2x2x4 slice. The times are simulated.
32 devices in a mesh: rows: 2 (over y), cols: 4 (over z), slabs: 2 (over x), trial: 2 (over core).
Axes of the slice: x: 2, y: 2, z: 4, core: 2. Of those that a mesh axis runs over, the one named last changes fastest.
Arguments:
- field_values: float32 [64, 16, 256, 128], P(('trial', 'rows'), 'cols', 'slabs'), parts along dimension 0, may hold values from 0.5 to 2
- conductance: float32 [64, 16, 256, 128], P(('trial', 'rows'), 'cols', 'slabs'), parts along dimension 0, may hold values from 0.03 to 0.15
- source: float32 [64, 16, 256, 128], P(('trial', 'rows'), 'cols', 'slabs'), parts along dimension 0, may hold values from -0.2 to 0.2
Outputs:
- anomaly: float32 [64, 16, 256, 128], P(('trial', 'rows'), 'cols', 'slabs'), parts along dimension 0
- field_values_end: float32 [64, 16, 256, 128], P(('trial', 'rows'), 'cols', 'slabs'), parts along dimension 0
There are 2 independent parts, one for each index of `trial`. A program takes and returns all parts, laid end to end along the dimension named above; each array names one. Nothing has to cross between parts.
All inputs are finite; a program needn't handle non-finite values.
Results may differ from a plain program's by a relative error of at most 0.00002.
Values sent between devices are 32-bit elements; how exact they have to be, the bound alone decides.
No kernel may reach another device: no remote copies, remote signals or barrier semaphores. Data moves between devices by JAX's collectives and lax.ppermute only.
A program may use at most 128 MiB of HBM per device.

v0:
```python
import jax
import jax.numpy as jnp
from jax import lax
from jax.sharding import PartitionSpec as P

STEPS = 4


def extended(cells, sides, width):
    for axis, dim in sides:
        count = lax.axis_size(axis)
        ends = count - 1
        head = lax.slice_in_dim(cells, 0, width, axis=dim)
        tail = lax.slice_in_dim(cells, cells.shape[dim] - width, cells.shape[dim], axis=dim)
        cells = jnp.concatenate(
            [
                lax.ppermute(tail, axis, [(i, (i + 1) % count) for i in range(ends)]),
                cells,
                lax.ppermute(head, axis, [((i + 1) % count, i) for i in range(ends)]),
            ],
            axis=dim,
        )
    return cells


def strip_edges(values, dims):
    for dim in dims:
        values = lax.slice_in_dim(values, 1, values.shape[dim] - 1, axis=dim)
    return values


def neighbour(values, dim, start, dims):
    others = [other for other in dims if other != dim]
    values = strip_edges(values, others)
    return lax.slice_in_dim(values, start, start + values.shape[dim] - 2, axis=dim)


def one_step(padded, conductance, source):
    middle = strip_edges(padded, (0, 1, 2))
    lower = [neighbour(padded, dim, 0, (0, 1, 2)) for dim in (0, 1, 2)]
    upper = [neighbour(padded, dim, 2, (0, 1, 2)) for dim in (0, 1, 2)]
    spread = lower[0] + upper[0] + lower[1] + upper[1] + lower[2] + upper[2] - 6.0 * middle
    return middle + conductance * spread + source


def on_device(field_values, conductance, source):
    for step in range(STEPS):
        padded = extended(field_values, (("rows", 0), ("cols", 1), ("slabs", 2)), 1)
        field_values = one_step(padded, conductance, source)
    count = field_values.shape[0] * lax.axis_size("rows")
    guess = 1.0
    moved = field_values - guess
    totals, squares = lax.psum(
        (jnp.sum(moved, axis=0, keepdims=True), jnp.sum(moved * moved, axis=0, keepdims=True)),
        "rows",
    )
    line_mean = guess + totals / count
    centred = field_values - line_mean
    line_variance = squares / count - totals / count * (totals / count)
    anomaly = centred * lax.rsqrt(line_variance + 0.0001)
    return (anomaly, field_values)


def solution(mesh):
    in_specs = (
        P(("trial", "rows"), "cols", "slabs", None),
        P(("trial", "rows"), "cols", "slabs", None),
        P(("trial", "rows"), "cols", "slabs", None),
    )
    out_specs = (
        P(("trial", "rows"), "cols", "slabs", None),
        P(("trial", "rows"), "cols", "slabs", None),
    )
    return jax.shard_map(
        on_device, mesh=mesh, in_specs=in_specs, out_specs=out_specs, check_vma=False
    )
```

profile of v0, /device:TPU:0, one launch (start us, length us, event | category | flops | bytes accessed | tf_op | source)
XLA Modules:
  0.0 269.4 jit_solution(2563802980039127332)
XLA Ops:
  8.3 4.9 %collective-permute-start = (f32[1,4,128,128]{3,2,1,0:T(8,128)S(1)}, f32[1,4,128,128]{3,2,1,0:T(8,128)S(1)}, u32[]{:S(2)}, u32[]{:S(2)}) collective-permute-start(f32[1,4,128,128]{3,2,1,0:T(8,128)S(1)} %get-tuple-element.30), channel_id=1, source_target_pairs={{0,16},{1,17},{2,18},{3,19},{4,20},{5,21},{6,22},{7,23},{8,24},{9,... | collective-permute-start | bytes 786440 | tf_op jit(solution)/shard_map/ppermute | solution.py:17
  14.5 4.2 %collective-permute-done = f32[1,4,128,128]{3,2,1,0:T(8,128)S(1)} collective-permute-done((f32[1,4,128,128]{3,2,1,0:T(8,128)S(1)}, f32[1,4,128,128]{3,2,1,0:T(8,128)S(1)}, u32[]{:S(2)}, u32[]{:S(2)}) %collective-permute-start) | collective-permute-done | bytes 262176 | tf_op jit(solution)/shard_map/ppermute | solution.py:17
  28.0 22.7 %collective-permute-done.2 = f32[18,1,128,128]{3,2,1,0:T(8,128)S(1)} collective-permute-done((f32[18,1,128,128]{3,2,1,0:T(8,128)S(1)}, f32[18,1,128,128]{3,2,1,0:T(8,128)S(1)}, u32[]{:S(2)}, u32[]{:S(2)}) %collective-permute-start.2) | collective-permute-done | bytes 1179680 | tf_op jit(solution)/shard_map/ppermute | solution.py:17
  50.7 4.2 %collective-permute-done.3 = f32[18,1,128,128]{3,2,1,0:T(8,128)S(1)} collective-permute-done((f32[18,1,128,128]{3,2,1,0:T(8,128)S(1)}, f32[18,1,128,128]{3,2,1,0:T(8,128)S(1)}, u32[]{:S(2)}, u32[]{:S(2)}) %collective-permute-start.3) | collective-permute-done | bytes 1179680 | tf_op jit(solution)/shard_map/ppermute | solution.py:19
  60.2 4.3 %collective-permute-done.5 = f32[18,6,1,128]{3,2,1,0:T(1,128)S(1)} collective-permute-done((f32[18,6,1,128]{3,2,1,0:T(1,128)S(1)}, f32[18,6,1,128]{3,2,1,0:T(1,128)S(1)}, u32[]{:S(2)}, u32[]{:S(2)}) %collective-permute-start.5) | collective-permute-done | bytes 55328 | tf_op jit(solution)/shard_map/ppermute | solution.py:19
  64.4 18.6 %fusion.31 = f32[16,4,128,128]{3,2,1,0:T(8,128)S(1)} fusion(f32[16,4,128,128]{3,2,1,0:T(8,128)} %param.5, f32[16,4,128,128]{3,2,1,0:T(8,128)} %param.3, f32[16,4,128,128]{3,2,1,0:T(8,128)} %param.4, f32[18,6,1,128]{3,2,1,0:T(1,128)S(1)} %collective-permute-done.5, f32[18,1,128,128]{3,2,1,0:T(8,128)S(1)} %collective-permute-done.3, ...), kind=kLoop, calls=%fused_computation.86 | loop fusion | flops 20971520 | bytes 24489984 | tf_op jit(solution)/shard_map/add | solution.py:43
  90.0 4.4 %collective-permute-done.7 = f32[1,4,128,128]{3,2,1,0:T(8,128)S(1)} collective-permute-done((f32[1,4,128,128]{3,2,1,0:T(8,128)S(1)}, f32[1,4,128,128]{3,2,1,0:T(8,128)S(1)}, u32[]{:S(2)}, u32[]{:S(2)}) %collective-permute-start.7) | collective-permute-done | bytes 262176 | tf_op jit(solution)/shard_map/ppermute | solution.py:19
  94.6 3.7 %collective-permute-start.8 = (f32[18,1,128,128]{3,2,1,0:T(8,128)S(1)}, f32[18,1,128,128]{3,2,1,0:T(8,128)S(1)}, u32[]{:S(2)}, u32[]{:S(2)}) collective-permute-start(f32[18,1,128,128]{3,2,1,0:T(8,128)S(1)} %get-tuple-element.19), channel_id=1, source_target_pairs={{0,4},{4,8},{8,12},{1,5},{5,9},{9,13},{2,6},{6,10},{10,14},{3,7},{... | collective-permute-start | bytes 3538952 | tf_op jit(solution)/shard_map/ppermute | solution.py:17
  99.6 19.0 %collective-permute-done.8 = f32[18,1,128,128]{3,2,1,0:T(8,128)S(1)} collective-permute-done((f32[18,1,128,128]{3,2,1,0:T(8,128)S(1)}, f32[18,1,128,128]{3,2,1,0:T(8,128)S(1)}, u32[]{:S(2)}, u32[]{:S(2)}) %collective-permute-start.8) | collective-permute-done | bytes 1179680 | tf_op jit(solution)/shard_map/ppermute | solution.py:17
  118.6 4.2 %collective-permute-done.9 = f32[18,1,128,128]{3,2,1,0:T(8,128)S(1)} collective-permute-done((f32[18,1,128,128]{3,2,1,0:T(8,128)S(1)}, f32[18,1,128,128]{3,2,1,0:T(8,128)S(1)}, u32[]{:S(2)}, u32[]{:S(2)}) %collective-permute-start.9) | collective-permute-done | bytes 1179680 | tf_op jit(solution)/shard_map/ppermute | solution.py:19
  126.6 4.3 %collective-permute-done.11 = f32[18,6,1,128]{3,2,1,0:T(1,128)S(1)} collective-permute-done((f32[18,6,1,128]{3,2,1,0:T(1,128)S(1)}, f32[18,6,1,128]{3,2,1,0:T(1,128)S(1)}, u32[]{:S(2)}, u32[]{:S(2)}) %collective-permute-start.11) | collective-permute-done | bytes 55328 | tf_op jit(solution)/shard_map/ppermute | solution.py:19
  130.8 5.5 %fusion.22 = f32[16,4,128,128]{3,2,1,0:T(8,128)S(1)} fusion(f32[16,4,128,128]{3,2,1,0:T(8,128)S(1)} %copy-done, f32[16,4,128,128]{3,2,1,0:T(8,128)S(1)} %fusion.31, f32[16,4,128,128]{3,2,1,0:T(8,128)S(1)} %copy-done.1, f32[18,6,1,128]{3,2,1,0:T(1,128)S(1)} %collective-permute-done.11, f32[18,1,128,128]{3,2,1,0:T(8,128)S(1)} %collective-permute-done.9, ...), kind=kLoop, calls=%fused_computation.59 | loop fusion | flops 29360128 | bytes 19771392 | tf_op jit(solution)/shard_map/add | solution.py:43
  142.0 4.4 %collective-permute-done.13 = f32[1,4,128,128]{3,2,1,0:T(8,128)S(1)} collective-permute-done((f32[1,4,128,128]{3,2,1,0:T(8,128)S(1)}, f32[1,4,128,128]{3,2,1,0:T(8,128)S(1)}, u32[]{:S(2)}, u32[]{:S(2)}) %collective-permute-start.13) | collective-permute-done | bytes 262176 | tf_op jit(solution)/shard_map/ppermute | solution.py:19
  151.4 15.6 %collective-permute-done.14 = f32[18,1,128,128]{3,2,1,0:T(8,128)S(1)} collective-permute-done((f32[18,1,128,128]{3,2,1,0:T(8,128)S(1)}, f32[18,1,128,128]{3,2,1,0:T(8,128)S(1)}, u32[]{:S(2)}, u32[]{:S(2)}) %collective-permute-start.14) | collective-permute-done | bytes 1179680 | tf_op jit(solution)/shard_map/ppermute | solution.py:17
  167.0 4.2 %collective-permute-done.15 = f32[18,1,128,128]{3,2,1,0:T(8,128)S(1)} collective-permute-done((f32[18,1,128,128]{3,2,1,0:T(8,128)S(1)}, f32[18,1,128,128]{3,2,1,0:T(8,128)S(1)}, u32[]{:S(2)}, u32[]{:S(2)}) %collective-permute-start.15) | collective-permute-done | bytes 1179680 | tf_op jit(solution)/shard_map/ppermute | solution.py:19
  174.9 4.3 %collective-permute-done.17 = f32[18,6,1,128]{3,2,1,0:T(1,128)S(1)} collective-permute-done((f32[18,6,1,128]{3,2,1,0:T(1,128)S(1)}, f32[18,6,1,128]{3,2,1,0:T(1,128)S(1)}, u32[]{:S(2)}, u32[]{:S(2)}) %collective-permute-start.17) | collective-permute-done | bytes 55328 | tf_op jit(solution)/shard_map/ppermute | solution.py:19
  179.2 5.7 %fusion.13 = f32[16,4,128,128]{3,2,1,0:T(8,128)S(1)} fusion(f32[16,4,128,128]{3,2,1,0:T(8,128)S(1)} %copy-done, f32[16,4,128,128]{3,2,1,0:T(8,128)S(1)} %fusion.22, f32[16,4,128,128]{3,2,1,0:T(8,128)S(1)} %copy-done.1, f32[18,6,1,128]{3,2,1,0:T(1,128)S(1)} %collective-permute-done.17, f32[18,1,128,128]{3,2,1,0:T(8,128)S(1)} %collective-permute-done.15, ...), kind=kLoop, calls=%fused_computation.32 | loop fusion | flops 29360128 | bytes 19771392 | tf_op jit(solution)/shard_map/add | solution.py:43
  190.6 4.4 %collective-permute-done.19 = f32[1,4,128,128]{3,2,1,0:T(8,128)S(1)} collective-permute-done((f32[1,4,128,128]{3,2,1,0:T(8,128)S(1)}, f32[1,4,128,128]{3,2,1,0:T(8,128)S(1)}, u32[]{:S(2)}, u32[]{:S(2)}) %collective-permute-start.19) | collective-permute-done | bytes 262176 | tf_op jit(solution)/shard_map/ppermute | solution.py:19
  199.1 12.7 %collective-permute-done.20 = f32[18,1,128,128]{3,2,1,0:T(8,128)S(1)} collective-permute-done((f32[18,1,128,128]{3,2,1,0:T(8,128)S(1)}, f32[18,1,128,128]{3,2,1,0:T(8,128)S(1)}, u32[]{:S(2)}, u32[]{:S(2)}) %collective-permute-start.20) | collective-permute-done | bytes 1179680 | tf_op jit(solution)/shard_map/ppermute | solution.py:17
  211.9 4.2 %collective-permute-done.21 = f32[18,1,128,128]{3,2,1,0:T(8,128)S(1)} collective-permute-done((f32[18,1,128,128]{3,2,1,0:T(8,128)S(1)}, f32[18,1,128,128]{3,2,1,0:T(8,128)S(1)}, u32[]{:S(2)}, u32[]{:S(2)}) %collective-permute-start.21) | collective-permute-done | bytes 1179680 | tf_op jit(solution)/shard_map/ppermute | solution.py:19
  219.5 4.3 %collective-permute-done.23 = f32[18,6,1,128]{3,2,1,0:T(1,128)S(1)} collective-permute-done((f32[18,6,1,128]{3,2,1,0:T(1,128)S(1)}, f32[18,6,1,128]{3,2,1,0:T(1,128)S(1)}, u32[]{:S(2)}, u32[]{:S(2)}) %collective-permute-start.23) | collective-permute-done | bytes 55328 | tf_op jit(solution)/shard_map/ppermute | solution.py:19
  223.8 7.5 %add_reduce_fusion = (f32[4,128,128]{2,1,0:T(8,128)}, f32[4,128,128]{2,1,0:T(8,128)}, f32[16,4,128,128]{3,2,1,0:T(8,128)}) fusion(f32[16,4,128,128]{3,2,1,0:T(8,128)S(1)} %copy-done, f32[16,4,128,128]{3,2,1,0:T(8,128)S(1)} %fusion.13, f32[16,4,128,128]{3,2,1,0:T(8,128)S(1)} %copy-done.1, f32[18,6,1,128]{3,2,1,0:T(1,128)S(1)} %collective-permute-done.23, ...), kind=kLoop, calls=%fused_computation.102 | loop fusion | flops 33423360 | bytes 20295680 | tf_op jit(solution)/shard_map/reduce_sum | solution.py:54
  231.4 25.1 %all-reduce.3.cloned.1.call-done = (f32[1,4,128,128]{3,2,1,0:T(8,128)}, f32[1,4,128,128]{3,2,1,0:T(8,128)}) async-done(((f32[1,4,128,128]{3,2,1,0:T(8,128)}, f32[1,4,128,128]{3,2,1,0:T(8,128)}), (f32[1,4,128,128]{3,2,1,0:T(8,128)}, f32[1,4,128,128]{3,2,1,0:T(8,128)})) %all-reduce.3.cloned.1.call-update) | async-done | bytes 524304 | tf_op jit(solution)/shard_map/psum | solution.py:53
  257.5 5.0 %subtract_multiply_fusion = f32[16,4,128,128]{3,2,1,0:T(8,128)} fusion(f32[16,4,128,128]{3,2,1,0:T(8,128)} %get-tuple-element.6, f32[4,128,128]{2,1,0:T(8,128)S(1)} %get-tuple-element.32, f32[4,128,128]{2,1,0:T(8,128)S(1)} %get-tuple-element.31), kind=kLoop, calls=%fused_computation.101 | loop fusion | flops 2097152 | bytes 8912896 | tf_op jit(solution)/shard_map/mul | solution.py:60
  (54 shorter events, 57.8 us)
Async XLA Ops:
  7.2 249.3 %all-reduce.3.cloned.1.call-start = ((), (), s32[]{:S(2)}) async-start(), calls=%async_computation | async-start | bytes 1048576 | tf_op jit(solution)/shard_map/psum | solution.py:53
  8.3 10.5 %collective-permute-start = (f32[1,4,128,128]{3,2,1,0:T(8,128)S(1)}, f32[1,4,128,128]{3,2,1,0:T(8,128)S(1)}, u32[]{:S(2)}, u32[]{:S(2)}) collective-permute-start(f32[1,4,128,128]{3,2,1,0:T(8,128)S(1)} %get-tuple-element.30), channel_id=1, source_target_pairs={{0,16},{1,17},{2,18},{3,19},{4,20},{5,21},{6,22},{7,23},{8,24},{9,... | collective-permute-start | bytes 786440 | tf_op jit(solution)/shard_map/ppermute | solution.py:17
  13.2 9.7 %collective-permute-start.1 = (f32[1,4,128,128]{3,2,1,0:T(8,128)S(1)}, f32[1,4,128,128]{3,2,1,0:T(8,128)S(1)}, u32[]{:S(2)}, u32[]{:S(2)}) collective-permute-start(f32[1,4,128,128]{3,2,1,0:T(8,128)S(1)} %get-tuple-element.29), channel_id=1, source_target_pairs={{16,0},{17,1},{18,2},{19,3},{20,4},{21,5},{22,6},{23,7},{24,8},{25... | collective-permute-start | bytes 786440 | tf_op jit(solution)/shard_map/ppermute | solution.py:19
  23.1 27.6 %collective-permute-start.2 = (f32[18,1,128,128]{3,2,1,0:T(8,128)S(1)}, f32[18,1,128,128]{3,2,1,0:T(8,128)S(1)}, u32[]{:S(2)}, u32[]{:S(2)}) collective-permute-start(f32[18,1,128,128]{3,2,1,0:T(8,128)S(1)} %get-tuple-element.21), channel_id=1, source_target_pairs={{0,4},{4,8},{8,12},{1,5},{5,9},{9,13},{2,6},{6,10},{10,14},{3,7},{... | collective-permute-start | bytes 3538952 | tf_op jit(solution)/shard_map/ppermute | solution.py:17
  26.7 28.2 %collective-permute-start.3 = (f32[18,1,128,128]{3,2,1,0:T(8,128)S(1)}, f32[18,1,128,128]{3,2,1,0:T(8,128)S(1)}, u32[]{:S(2)}, u32[]{:S(2)}) collective-permute-start(f32[18,1,128,128]{3,2,1,0:T(8,128)S(1)} %get-tuple-element.22), channel_id=1, source_target_pairs={{4,0},{8,4},{12,8},{5,1},{9,5},{13,9},{6,2},{10,6},{14,10},{7,3},{... | collective-permute-start | bytes 3538952 | tf_op jit(solution)/shard_map/ppermute | solution.py:19
  55.0 5.2 %collective-permute-start.4 = (f32[18,6,1,128]{3,2,1,0:T(1,128)S(1)}, f32[18,6,1,128]{3,2,1,0:T(1,128)S(1)}, u32[]{:S(2)}, u32[]{:S(2)}) collective-permute-start(f32[18,6,1,128]{3,2,1,0:T(1,128)S(1)} %get-tuple-element.13), channel_id=1, source_target_pairs={{0,2},{1,3},{4,6},{5,7},{8,10},{9,11},{12,14},{13,15},{16,18},{17,... | collective-permute-start | bytes 165896 | tf_op jit(solution)/shard_map/ppermute | solution.py:17
  58.4 6.0 %collective-permute-start.5 = (f32[18,6,1,128]{3,2,1,0:T(1,128)S(1)}, f32[18,6,1,128]{3,2,1,0:T(1,128)S(1)}, u32[]{:S(2)}, u32[]{:S(2)}) collective-permute-start(f32[18,6,1,128]{3,2,1,0:T(1,128)S(1)} %get-tuple-element.14), channel_id=1, source_target_pairs={{2,0},{3,1},{6,4},{7,5},{10,8},{11,9},{14,12},{15,13},{18,16},{19,... | collective-permute-start | bytes 165896 | tf_op jit(solution)/shard_map/ppermute | solution.py:19
  83.1 6.9 %collective-permute-start.6 = (f32[1,4,128,128]{3,2,1,0:T(8,128)S(1)}, f32[1,4,128,128]{3,2,1,0:T(8,128)S(1)}, u32[]{:S(2)}, u32[]{:S(2)}) collective-permute-start(f32[1,4,128,128]{3,2,1,0:T(8,128)S(1)} %get-tuple-element.27), channel_id=1, source_target_pairs={{0,16},{1,17},{2,18},{3,19},{4,20},{5,21},{6,22},{7,23},{8,24},{9,... | collective-permute-start | bytes 786440 | tf_op jit(solution)/shard_map/ppermute | solution.py:17
  86.1 8.3 %collective-permute-start.7 = (f32[1,4,128,128]{3,2,1,0:T(8,128)S(1)}, f32[1,4,128,128]{3,2,1,0:T(8,128)S(1)}, u32[]{:S(2)}, u32[]{:S(2)}) collective-permute-start(f32[1,4,128,128]{3,2,1,0:T(8,128)S(1)} %get-tuple-element.28), channel_id=1, source_target_pairs={{16,0},{17,1},{18,2},{19,3},{20,4},{21,5},{22,6},{23,7},{24,8},{25... | collective-permute-start | bytes 786440 | tf_op jit(solution)/shard_map/ppermute | solution.py:19
  94.6 24.0 %collective-permute-start.8 = (f32[18,1,128,128]{3,2,1,0:T(8,128)S(1)}, f32[18,1,128,128]{3,2,1,0:T(8,128)S(1)}, u32[]{:S(2)}, u32[]{:S(2)}) collective-permute-start(f32[18,1,128,128]{3,2,1,0:T(8,128)S(1)} %get-tuple-element.19), channel_id=1, source_target_pairs={{0,4},{4,8},{8,12},{1,5},{5,9},{9,13},{2,6},{6,10},{10,14},{3,7},{... | collective-permute-start | bytes 3538952 | tf_op jit(solution)/shard_map/ppermute | solution.py:17
  98.3 24.5 %collective-permute-start.9 = (f32[18,1,128,128]{3,2,1,0:T(8,128)S(1)}, f32[18,1,128,128]{3,2,1,0:T(8,128)S(1)}, u32[]{:S(2)}, u32[]{:S(2)}) collective-permute-start(f32[18,1,128,128]{3,2,1,0:T(8,128)S(1)} %get-tuple-element.20), channel_id=1, source_target_pairs={{4,0},{8,4},{12,8},{5,1},{9,5},{13,9},{6,2},{10,6},{14,10},{7,3},{... | collective-permute-start | bytes 3538952 | tf_op jit(solution)/shard_map/ppermute | solution.py:19
  122.9 3.7 %collective-permute-start.10 = (f32[18,6,1,128]{3,2,1,0:T(1,128)S(1)}, f32[18,6,1,128]{3,2,1,0:T(1,128)S(1)}, u32[]{:S(2)}, u32[]{:S(2)}) collective-permute-start(f32[18,6,1,128]{3,2,1,0:T(1,128)S(1)} %get-tuple-element.11), channel_id=1, source_target_pairs={{0,2},{1,3},{4,6},{5,7},{8,10},{9,11},{12,14},{13,15},{16,18},{17,... | collective-permute-start | bytes 165896 | tf_op jit(solution)/shard_map/ppermute | solution.py:17
  124.8 6.0 %collective-permute-start.11 = (f32[18,6,1,128]{3,2,1,0:T(1,128)S(1)}, f32[18,6,1,128]{3,2,1,0:T(1,128)S(1)}, u32[]{:S(2)}, u32[]{:S(2)}) collective-permute-start(f32[18,6,1,128]{3,2,1,0:T(1,128)S(1)} %get-tuple-element.12), channel_id=1, source_target_pairs={{2,0},{3,1},{6,4},{7,5},{10,8},{11,9},{14,12},{15,13},{18,16},{19,... | collective-permute-start | bytes 165896 | tf_op jit(solution)/shard_map/ppermute | solution.py:19
  136.3 5.6 %collective-permute-start.12 = (f32[1,4,128,128]{3,2,1,0:T(8,128)S(1)}, f32[1,4,128,128]{3,2,1,0:T(8,128)S(1)}, u32[]{:S(2)}, u32[]{:S(2)}) collective-permute-start(f32[1,4,128,128]{3,2,1,0:T(8,128)S(1)} %get-tuple-element.25), channel_id=1, source_target_pairs={{0,16},{1,17},{2,18},{3,19},{4,20},{5,21},{6,22},{7,23},{8,24},{9,... | collective-permute-start | bytes 786440 | tf_op jit(solution)/shard_map/ppermute | solution.py:17
  138.1 8.3 %collective-permute-start.13 = (f32[1,4,128,128]{3,2,1,0:T(8,128)S(1)}, f32[1,4,128,128]{3,2,1,0:T(8,128)S(1)}, u32[]{:S(2)}, u32[]{:S(2)}) collective-permute-start(f32[1,4,128,128]{3,2,1,0:T(8,128)S(1)} %get-tuple-element.26), channel_id=1, source_target_pairs={{16,0},{17,1},{18,2},{19,3},{20,4},{21,5},{22,6},{23,7},{24,8},{25... | collective-permute-start | bytes 786440 | tf_op jit(solution)/shard_map/ppermute | solution.py:19
  146.6 20.4 %collective-permute-start.14 = (f32[18,1,128,128]{3,2,1,0:T(8,128)S(1)}, f32[18,1,128,128]{3,2,1,0:T(8,128)S(1)}, u32[]{:S(2)}, u32[]{:S(2)}) collective-permute-start(f32[18,1,128,128]{3,2,1,0:T(8,128)S(1)} %get-tuple-element.17), channel_id=1, source_target_pairs={{0,4},{4,8},{8,12},{1,5},{5,9},{9,13},{2,6},{6,10},{10,14},{3,7},{... | collective-permute-start | bytes 3538952 | tf_op jit(solution)/shard_map/ppermute | solution.py:17
  150.1 21.1 %collective-permute-start.15 = (f32[18,1,128,128]{3,2,1,0:T(8,128)S(1)}, f32[18,1,128,128]{3,2,1,0:T(8,128)S(1)}, u32[]{:S(2)}, u32[]{:S(2)}) collective-permute-start(f32[18,1,128,128]{3,2,1,0:T(8,128)S(1)} %get-tuple-element.18), channel_id=1, source_target_pairs={{4,0},{8,4},{12,8},{5,1},{9,5},{13,9},{6,2},{10,6},{14,10},{7,3},{... | collective-permute-start | bytes 3538952 | tf_op jit(solution)/shard_map/ppermute | solution.py:19
  171.3 3.7 %collective-permute-start.16 = (f32[18,6,1,128]{3,2,1,0:T(1,128)S(1)}, f32[18,6,1,128]{3,2,1,0:T(1,128)S(1)}, u32[]{:S(2)}, u32[]{:S(2)}) collective-permute-start(f32[18,6,1,128]{3,2,1,0:T(1,128)S(1)} %get-tuple-element.9), channel_id=1, source_target_pairs={{0,2},{1,3},{4,6},{5,7},{8,10},{9,11},{12,14},{13,15},{16,18},{17,... | collective-permute-start | bytes 165896 | tf_op jit(solution)/shard_map/ppermute | solution.py:17
  173.2 6.0 %collective-permute-start.17 = (f32[18,6,1,128]{3,2,1,0:T(1,128)S(1)}, f32[18,6,1,128]{3,2,1,0:T(1,128)S(1)}, u32[]{:S(2)}, u32[]{:S(2)}) collective-permute-start(f32[18,6,1,128]{3,2,1,0:T(1,128)S(1)} %get-tuple-element.10), channel_id=1, source_target_pairs={{2,0},{3,1},{6,4},{7,5},{10,8},{11,9},{14,12},{15,13},{18,16},{19,... | collective-permute-start | bytes 165896 | tf_op jit(solution)/shard_map/ppermute | solution.py:19
  184.9 5.6 %collective-permute-start.18 = (f32[1,4,128,128]{3,2,1,0:T(8,128)S(1)}, f32[1,4,128,128]{3,2,1,0:T(8,128)S(1)}, u32[]{:S(2)}, u32[]{:S(2)}) collective-permute-start(f32[1,4,128,128]{3,2,1,0:T(8,128)S(1)} %get-tuple-element.23), channel_id=1, source_target_pairs={{0,16},{1,17},{2,18},{3,19},{4,20},{5,21},{6,22},{7,23},{8,24},{9,... | collective-permute-start | bytes 786440 | tf_op jit(solution)/shard_map/ppermute | solution.py:17
  186.7 8.3 %collective-permute-start.19 = (f32[1,4,128,128]{3,2,1,0:T(8,128)S(1)}, f32[1,4,128,128]{3,2,1,0:T(8,128)S(1)}, u32[]{:S(2)}, u32[]{:S(2)}) collective-permute-start(f32[1,4,128,128]{3,2,1,0:T(8,128)S(1)} %get-tuple-element.24), channel_id=1, source_target_pairs={{16,0},{17,1},{18,2},{19,3},{20,4},{21,5},{22,6},{23,7},{24,8},{25... | collective-permute-start | bytes 786440 | tf_op jit(solution)/shard_map/ppermute | solution.py:19
  195.2 16.7 %collective-permute-start.20 = (f32[18,1,128,128]{3,2,1,0:T(8,128)S(1)}, f32[18,1,128,128]{3,2,1,0:T(8,128)S(1)}, u32[]{:S(2)}, u32[]{:S(2)}) collective-permute-start(f32[18,1,128,128]{3,2,1,0:T(8,128)S(1)} %get-tuple-element.15), channel_id=1, source_target_pairs={{0,4},{4,8},{8,12},{1,5},{5,9},{9,13},{2,6},{6,10},{10,14},{3,7},{... | collective-permute-start | bytes 3538952 | tf_op jit(solution)/shard_map/ppermute | solution.py:17
  197.8 18.2 %collective-permute-start.21 = (f32[18,1,128,128]{3,2,1,0:T(8,128)S(1)}, f32[18,1,128,128]{3,2,1,0:T(8,128)S(1)}, u32[]{:S(2)}, u32[]{:S(2)}) collective-permute-start(f32[18,1,128,128]{3,2,1,0:T(8,128)S(1)} %get-tuple-element.16), channel_id=1, source_target_pairs={{4,0},{8,4},{12,8},{5,1},{9,5},{13,9},{6,2},{10,6},{14,10},{7,3},{... | collective-permute-start | bytes 3538952 | tf_op jit(solution)/shard_map/ppermute | solution.py:19
  217.8 6.0 %collective-permute-start.23 = (f32[18,6,1,128]{3,2,1,0:T(1,128)S(1)}, f32[18,6,1,128]{3,2,1,0:T(1,128)S(1)}, u32[]{:S(2)}, u32[]{:S(2)}) collective-permute-start(f32[18,6,1,128]{3,2,1,0:T(1,128)S(1)} %get-tuple-element.8), channel_id=1, source_target_pairs={{2,0},{3,1},{6,4},{7,5},{10,8},{11,9},{14,12},{15,13},{18,16},{19,... | collective-permute-start | bytes 165896 | tf_op jit(solution)/shard_map/ppermute | solution.py:19
  (4 other events, 108.2 us)
Sparse Core Ops, SparseCore 0:
  231.5 24.9 all-reduce.2
where the time goes:
time: 270 us; the launch traced here: 269 us
  waiting for transfers between devices  158 us (59%)
  starting transfers between devices  49.2 us (18%)
  other arithmetic  44.3 us (16%)
  between operations  14.4 us (5%)
  local copies, waits for them, and re-layouts  3.93 us (1%)
    ppermute x12, waiting for transfers between devices, extended(): lax.ppermute(tail, axis, [(i, (i + 1) % count) for i in range(ends)])  83.9 us
    ppermute x12, waiting for transfers between devices, extended(): lax.ppermute(head, axis, [((i + 1) % count, i) for i in range(ends)])  48.7 us
    ppermute x12, starting transfers between devices, extended(): lax.ppermute(tail, axis, [(i, (i + 1) % count) for i in range(ends)])  33.6 us
    add x3, other arithmetic, one_step(): return middle + conductance * spread + source  29.7 us
    psum x1, waiting for transfers between devices, on_device(): lax.psum((jnp.sum(moved, axis=0, keepdims=True), jnp.sum(moved * moved, a...  25.1 us
    ppermute x12, starting transfers between devices, extended(): lax.ppermute(head, axis, [((i + 1) % count, i) for i in range(ends)])  15.5 us
    reduce_sum x1, other arithmetic, on_device(): jnp.sum(moved, axis=0, keepdims=True)  7.53 us
  transfers between devices with their start and end apart: 25, of which 25 were waited for; matrix products, arithmetic and copies ran while one was open for 1% of the time, Pallas kernels for 0%

commit v1 on v0

v1 whole, which is shorter than its diff:
```python
import jax
import jax.numpy as jnp
from jax import lax
from jax.experimental import pallas as pl
from jax.experimental.pallas import tpu as pltpu
from jax.sharding import PartitionSpec as P

STEPS = 4
CHUNKS = 2
ROWS = 8
HBM = pl.BlockSpec(memory_space=pltpu.HBM)
VMEM = pl.BlockSpec(memory_space=pltpu.VMEM)
F32 = jnp.float32


def vmem(*shape):
    return pltpu.VMEM(shape, F32)


def call(body, ins, in_specs, outs, out_specs, name, scratch=(), aliases=None, flops=0):
    return pl.pallas_call(
        body,
        in_specs=in_specs,
        out_shape=outs,
        out_specs=out_specs,
        scratch_shapes=scratch,
        input_output_aliases=aliases or {},
        compiler_params=pltpu.CompilerParams(vmem_limit_bytes=12 * 2**20),
        cost_estimate=pl.CostEstimate(flops=flops, bytes_accessed=0, transcendentals=0) if flops else None,
        name=name,
    )(*ins)


def ports_of(axis):
    return ("swap",) if lax.axis_size(axis) == 2 else ("up", "down")


def exchange(buffers, axis, ports=None):
    count = lax.axis_size(axis)
    perms = {
        "swap": [(0, 1), (1, 0)],
        "up": [(i, i + 1) for i in range(count - 1)],
        "down": [(i + 1, i) for i in range(count - 1)],
    }
    return [lax.ppermute(buffer, axis, perms[port]) for buffer, port in zip(buffers, ports or ports_of(axis))]


def sent_index(axis, port, extent):
    if port == "swap":
        return (1 - lax.axis_index(axis)) * (extent - 1)
    return extent - 1 if port == "up" else 0


def halo_readers(axis, refs):
    if len(refs) == 1:
        at = lax.axis_index(axis)
        has_lower = at.astype(F32)
        has_upper = (1 - at).astype(F32)
        return (lambda where: refs[0][where] * has_lower), (lambda where: refs[0][where] * has_upper)
    return (lambda where: refs[0][where]), (lambda where: refs[1][where])


def run_copies(copies):
    for copy in copies:
        copy.start()
    for copy in copies:
        copy.wait()


def first_faces(field, spans):
    J, I, K, L = field.shape
    y_ports, x_ports = ports_of("rows"), ports_of("slabs")

    def body(u, *refs):
        outs, sems = refs[:-1], refs[-1]
        outs = list(outs)
        pairs = []
        for k0, kc in spans:
            pairs.append((u.at[:, I - 1, pl.ds(k0, kc)], outs.pop(0)))
            pairs.append((u.at[:, 0, pl.ds(k0, kc)], outs.pop(0)))
        for k0, kc in spans:
            for port in y_ports:
                pairs.append((u.at[sent_index("rows", port, J), :, pl.ds(k0, kc)], outs.pop(0)))
        for port in x_ports:
            pairs.append((u.at[:, :, sent_index("slabs", port, K)], outs.pop(0)))
        run_copies([pltpu.make_async_copy(src, dst, sems.at[n]) for n, (src, dst) in enumerate(pairs)])

    shapes = []
    for _, kc in spans:
        shapes += [vmem(J, kc, L)] * 2
    for _, kc in spans:
        shapes += [vmem(I, kc, L)] * len(y_ports)
    shapes += [vmem(J, I, L)] * len(x_ports)
    outs = list(
        call(body, [field], [HBM], shapes, [VMEM] * len(shapes), "first_faces", [pltpu.SemaphoreType.DMA((len(shapes),))])
    )
    z = [[outs.pop(0), outs.pop(0)] for _ in spans]
    y = [[outs.pop(0) for _ in y_ports] for _ in spans]
    return z, y, outs


def load(arrays, spans):
    J, I, K, L = arrays[0].shape

    def body(*refs):
        ins, outs, sems = refs[: len(arrays)], refs[len(arrays) : -1], refs[-1]
        copies = []
        for n, ref in enumerate(ins):
            for m, (k0, kc) in enumerate(spans):
                at = n * len(spans) + m
                copies.append(pltpu.make_async_copy(ref.at[:, :, pl.ds(k0, kc)], outs[at], sems.at[at]))
        run_copies(copies)

    shapes = [vmem(J, I, kc, L) for _ in arrays for _, kc in spans]
    outs = call(
        body, arrays, [HBM] * len(arrays), shapes, [VMEM] * len(shapes), "load", [pltpu.SemaphoreType.DMA((len(shapes),))]
    )
    return [outs[n * len(spans) : (n + 1) * len(spans)] for n in range(len(arrays))]


def step(q, fields, cond, src, z_in, y_in, x_in, layers, last, newer):
    J, I, kc, L = fields[q].shape
    n_chunks = len(fields)
    z_in = z_in if z_in is not None else []
    y_ports, x_ports = ports_of("rows"), ports_of("slabs")
    send_x = not last and q == n_chunks - 1
    below = fields[q - 1] if q > 0 else None
    above = fields[q + 1] if q + 1 < n_chunks else None
    ins = [fields[q], cond, src] + [a for a in (below, above) if a is not None] + list(z_in) + list(y_in) + list(x_in)
    if send_x:
        ins.append(newer)
    nl = len(layers)

    def body(*refs):
        refs = list(refs)
        u, c, s = refs.pop(0), refs.pop(0), refs.pop(0)
        lower_u = refs.pop(0) if below is not None else None
        upper_u = refs.pop(0) if above is not None else None
        z = [refs.pop(0) for _ in z_in]
        y = [refs.pop(0) for _ in y_in]
        x = [refs.pop(0) for _ in x_in]
        first_u = refs.pop(0) if send_x else None
        out = refs.pop(0)
        y_lo, y_hi = halo_readers("rows", y)
        x_lo, x_hi = halo_readers("slabs", x)
        sublane = lax.broadcasted_iota(jnp.int32, (ROWS, L), 0)

        def tile(k, at_low, at_high):
            here = pl.ds(k, ROWS)
            known = {}

            def cells(j, i):
                if (j, i) not in known:
                    if j < 0:
                        known[j, i] = y_lo((i, here))
                    elif j >= J:
                        known[j, i] = y_hi((i, here))
                    elif i < 0:
                        known[j, i] = z[0][j, here]
                    elif i >= I:
                        known[j, i] = z[1][j, here]
                    else:
                        known[j, i] = u[j, i, here]
                return known[j, i]

            def edge_row(ref, j, i, row):
                return jnp.broadcast_to(ref[j, i, pl.ds(row, 1)], (ROWS, L))

            def k_lower(j, i):
                if not at_low:
                    return u[j, i, pl.ds(k - 1, ROWS)]
                if lower_u is not None:
                    edge = edge_row(lower_u, j, i, lower_u.shape[2] - 1)
                else:
                    edge = jnp.broadcast_to(x_lo((j, pl.ds(i, 1))), (ROWS, L))
                return jnp.where(sublane == 0, edge, pltpu.roll(cells(j, i), 1, 0))

            def k_upper(j, i):
                if not at_high:
                    return u[j, i, pl.ds(k + 1, ROWS)]
                if upper_u is not None:
                    edge = edge_row(upper_u, j, i, 0)
                else:
                    edge = jnp.broadcast_to(x_hi((j, pl.ds(i, 1))), (ROWS, L))
                return jnp.where(sublane == ROWS - 1, edge, pltpu.roll(cells(j, i), ROWS - 1, 0))

            totals = [None] * nl
            for j in range(J):
                for n, i in enumerate(layers):
                    middle = cells(j, i)
                    spread = (
                        (cells(j - 1, i) + cells(j + 1, i))
                        + (cells(j, i - 1) + cells(j, i + 1))
                        + (k_lower(j, i) + k_upper(j, i))
                        - 6.0 * middle
                    )
                    new = middle + c[j, i, here] * spread + s[j, i, here]
                    out[j, n, here] = new
                    if last:
                        totals[n] = new if j == 0 else totals[n] + new
                    else:
                        if i == I - 1:
                            z_up[j, here] = new
                        if i == 0:
                            z_down[j, here] = new
                for i in list(known):
                    if i[0] < j:
                        del known[i]
            if last:
                for n in range(nl):
                    mean = totals[n] * (1.0 / J)
                    spread = None
                    for j in range(J):
                        off = out[j, n, here] - mean
                        spread = off * off if j == 0 else spread + off * off
                    stats[0, n, here] = mean
                    stats[1, n, here] = spread

        if last:
            stats = refs.pop(0)
        else:
            z_up, z_down = refs.pop(0), refs.pop(0)
            y_out = [refs.pop(0) for _ in y_ports]
            x_out = [refs.pop(0) for _ in x_ports] if send_x else []

        tiles = kc // ROWS
        tile(0, True, tiles == 1)
        if tiles > 2:

            def inner(t, carry):
                tile(pl.multiple_of(t * ROWS, ROWS), False, False)
                return carry

            lax.fori_loop(1, tiles - 1, inner, 0)
        if tiles > 1:
            tile(kc - ROWS, False, True)
        if not last:
            for ref, port in zip(y_out, y_ports):
                ref[...] = out[sent_index("rows", port, J)]
            for ref, port in zip(x_out, x_ports):
                for j in range(J):
                    head = first_u[j, :, 0, :]
                    tail = out[j, :, kc - 1, :]
                    if port == "swap":
                        at = lax.axis_index("slabs").astype(F32)
                        ref[j] = head * at + tail * (1.0 - at)
                    else:
                        ref[j] = tail if port == "up" else head

    shapes = [vmem(J, nl, kc, L)]
    if last:
        shapes.append(vmem(2, nl, kc, L))
    else:
        shapes += [vmem(J, kc, L)] * 2 + [vmem(I, kc, L)] * len(y_ports)
        if send_x:
            shapes += [vmem(J, I, L)] * len(x_ports)
    outs = list(
        call(
            body,
            ins,
            [VMEM] * len(ins),
            shapes,
            [VMEM] * len(shapes),
            f"step_{'last' if last else 'mid'}_{q}_{'_'.join(map(str, layers))}",
            flops=10 * J * nl * kc * L,
        )
    )
    new = outs.pop(0)
    if last:
        return new, outs[0]
    z = [outs.pop(0), outs.pop(0)]
    y = [outs.pop(0) for _ in y_ports]
    return new, z, y, outs


def finish(new, own, others, layers, span, buffers, shape):
    J, I, K, L = shape
    k0, kc = span
    nl = len(layers)
    count = len(others) + 1

    def body(*refs):
        refs = list(refs)
        u = refs.pop(0)
        sums = [refs.pop(0) for _ in range(count)]
        if buffers:
            refs.pop(0), refs.pop(0)
        anomaly_out, field_out, scaled, sems = refs
        copies = []
        for n, i in enumerate(layers):
            copies.append(pltpu.make_async_copy(u.at[:, n], field_out.at[:, i, pl.ds(k0, kc)], sems.at[n]))
            copies[-1].start()

        for n, i in enumerate(layers):

            def tile(t, carry):
                here = pl.ds(pl.multiple_of(t * ROWS, ROWS), ROWS)
                means = [ref[0, n, here] for ref in sums]
                mean = means[0]
                for other in means[1:]:
                    mean = mean + other
                mean = mean * (1.0 / count)
                spread = None
                for ref, own_mean in zip(sums, means):
                    off = own_mean - mean
                    part = ref[1, n, here] + J * (off * off)
                    spread = part if spread is None else spread + part
                scale = lax.rsqrt(spread * (1.0 / (J * count)) + 0.0001)
                for j in range(J):
                    scaled[j, n, here] = (u[j, n, here] - mean) * scale
                return carry

            lax.fori_loop(0, kc // ROWS, tile, 0)
            copies.append(pltpu.make_async_copy(scaled.at[:, n], anomaly_out.at[:, i, pl.ds(k0, kc)], sems.at[nl + n]))
            copies[-1].start()
        for copy in copies:
            copy.wait()

    full = jax.ShapeDtypeStruct(shape, F32)
    ins = [new, own] + list(others)
    aliases = {len(ins): 0, len(ins) + 1: 1} if buffers else {}
    return call(
        body,
        ins + list(buffers),
        [VMEM] * len(ins) + [HBM] * len(buffers),
        [full, full],
        [HBM, HBM],
        f"finish_{k0}_{'_'.join(map(str, layers))}",
        [pltpu.VMEM((J, nl, kc, L), F32), pltpu.SemaphoreType.DMA((2 * nl,))],
        aliases,
        flops=10 * J * nl * kc * L,
    )


def other_rows(own):
    count = lax.axis_size("rows")
    return [lax.ppermute(own, "rows", [(i, (i + shift) % count) for i in range(count)]) for shift in range(1, count)]


def spans_of(extent):
    tiles = extent // ROWS
    cuts = [tiles * n // CHUNKS * ROWS for n in range(CHUNKS + 1)]
    return [(a, b - a) for a, b in zip(cuts, cuts[1:])]


def on_device(field_values, conductance, source):
    shape = J, I, K, L = field_values.shape
    spans = spans_of(K)
    chunks = range(len(spans))
    z_out, y_out, x_out = first_faces(field_values, spans)
    z_in = [exchange(z_out[q], "cols", ("up", "down")) for q in chunks]
    y_in = [exchange(y_out[q], "rows") for q in chunks]
    x_in = exchange(x_out, "slabs")
    fields, cond, src = load([field_values, conductance, source], spans)
    for _ in range(STEPS - 1):
        newer, z_next, y_next = [], [], []
        for q in chunks:
            new, z, y, x_out = step(
                q, fields, cond[q], src[q], z_in[q], y_in[q], x_in, range(I), False, newer[0] if newer else None
            )
            newer.append(new)
            z_next.append(exchange(z, "cols", ("up", "down")))
            y_next.append(exchange(y, "rows"))
        x_in = exchange(x_out, "slabs")
        fields, z_in, y_in = newer, z_next, y_next

    buffers = []
    inner, outer = list(range(1, I - 1)), [0, I - 1]
    parts = [(inner, q) for q in chunks] + [(outer, q) for q in chunks]
    for layers, q in parts:
        faces = z_in[q] if layers is outer else None
        new, own = step(q, fields, cond[q], src[q], faces, y_in[q], x_in, layers, True, None)
        buffers = finish(new, own, other_rows(own), layers, spans[q], buffers, shape)
    return tuple(buffers)


def solution(mesh):
    spec = P(("trial", "rows"), "cols", "slabs", None)
    return jax.shard_map(
        on_device, mesh=mesh, in_specs=(spec, spec, spec), out_specs=(spec, spec), check_vma=False
    )
```

time: 270 us -> 127 us (0.47)
  waiting for transfers between devices: 158 us -> 31 us
  other arithmetic: 44.3 us -> 0 us
  Pallas kernels: 0 us -> 24.4 us
  starting transfers between devices: 49.2 us -> 66 us
  between operations: 14.4 us -> 1.01 us
    ppermute x24 -> x32, waiting for transfers between devices: 133 us -> 31 us  [the longest x28 31 us: exchange(): lax.ppermute(buffer, axis, perms[port])]
    add x3 -> x0, other arithmetic: 29.7 us -> none  [one_step(): return middle + conductance * spread + source]
    psum x1 -> x0, waiting for transfers between devices: 25.1 us -> none  [on_device(): lax.psum((jnp.sum(moved, axis=0, keepdims=True), jnp.sum(moved * moved, a...]
    pallas_call x0 -> x16, Pallas kernels: none -> 24.4 us  [call(): pl.pallas_call(body, in_specs=in_specs, out_shape=outs, out_specs=out_spe...]
    ppermute x24 -> x32, starting transfers between devices: 49.2 us -> 66 us  [the longest x28 61.7 us: exchange(): lax.ppermute(buffer, axis, perms[port])]
    reduce_sum x1 -> x0, other arithmetic: 7.53 us -> none  [on_device(): jnp.sum(moved, axis=0, keepdims=True)]
    mul x1 -> x0, other arithmetic: 4.99 us -> none  [on_device(): anomaly = centred * lax.rsqrt(line_variance + 0.0001)]
  transfers between devices with their start and end apart: 25 -> 32, of which waited for: 25 -> 9; matrix products, arithmetic and copies ran while one was open for 1% -> 0% of each run, Pallas kernels for 0% -> 18%
where the time goes in v1:
time: 127 us
  starting transfers between devices  66 us (52%)
  waiting for transfers between devices  31 us (24%)
  Pallas kernels  24.4 us (19%)
  local copies, waits for them, and re-layouts  4.37 us (3%)
    ppermute x28, starting transfers between devices, exchange(): lax.ppermute(buffer, axis, perms[port])  61.7 us
    ppermute x28, waiting for transfers between devices, exchange(): lax.ppermute(buffer, axis, perms[port])  31 us
    pallas_call x16, Pallas kernels, call(): pl.pallas_call(body, in_specs=in_specs, out_shape=outs, out_specs=out_spe...  24.4 us
    unnamed x6, local copies, waits for them, and re-layouts  4.37 us
    ppermute x4, starting transfers between devices, other_rows(): lax.ppermute(own, 'rows', [(i, (i + shift) % count) for i in range(count)])  4.24 us
  transfers between devices with their start and end apart: 32, of which 9 were waited for; matrix products, arithmetic and copies ran while one was open for 0% of the time, Pallas kernels for 18%

profile of v1, /device:TPU:0, one launch (start us, length us, event | category | flops | bytes accessed | tf_op | source)
XLA Modules:
  0.0 126.8 jit_solution(11781717604012006704)
XLA Ops:
  0.6 2.2 %copy-done = f32[16,4,128,128]{3,2,1,0:T(8,128)S(1)} copy-done((f32[16,4,128,128]{3,2,1,0:T(8,128)S(1)}, f32[16,4,128,128]{3,2,1,0:T(8,128)}, u32[]{:S(2)}) %copy-start) | copy-done | bytes 4194328
  3.2 5.3 %collective-permute-start.4 = (f32[16,64,128]{2,1,0:T(8,128)S(1)}, f32[16,64,128]{2,1,0:T(8,128)S(1)}, u32[]{:S(2)}, u32[]{:S(2)}) collective-permute-start(f32[16,64,128]{2,1,0:T(8,128)S(1)} %get-tuple-element.66), channel_id=1, source_target_pairs={{0,4},{4,8},{8,12},{1,5},{5,9},{9,13},{2,6},{6,10},{10,14},{3,7},{... | collective-permute-start | bytes 1572872 | tf_op jit(solution)/shard_map/ppermute | solution.py:45
  9.7 4.6 %collective-permute-start = (f32[16,64,128]{2,1,0:T(8,128)S(1)}, f32[16,64,128]{2,1,0:T(8,128)S(1)}, u32[]{:S(2)}, u32[]{:S(2)}) collective-permute-start(f32[16,64,128]{2,1,0:T(8,128)S(1)} %get-tuple-element.60), channel_id=1, source_target_pairs={{0,4},{4,8},{8,12},{1,5},{5,9},{9,13},{2,6},{6,10},{10,14},{3,7},{... | collective-permute-start | bytes 1572872 | tf_op jit(solution)/shard_map/ppermute | solution.py:45
  17.2 2.4 %collective-permute-done.3.refs_7_ = f32[16,4,128]{2,1,0:T(4,128)S(1)} collective-permute-done((f32[16,4,128]{2,1,0:T(4,128)S(1)}, f32[16,4,128]{2,1,0:T(4,128)S(1)}, u32[]{:S(2)}, u32[]{:S(2)}) %collective-permute-start.3) | collective-permute-done | bytes 32800 | tf_op jit(solution)/shard_map/ppermute | solution.py:45
  21.1 3.6 %collective-permute-done.6.refs_6_ = f32[4,64,128]{2,1,0:T(8,128)S(1)} collective-permute-done((f32[4,64,128]{2,1,0:T(8,128)S(1)}, f32[4,64,128]{2,1,0:T(8,128)S(1)}, u32[]{:S(2)}, u32[]{:S(2)}) %collective-permute-start.6) | collective-permute-done | bytes 131104 | tf_op jit(solution)/shard_map/ppermute | solution.py:45
  26.2 2.2 %copy-done.2 = f32[16,4,128,128]{3,2,1,0:T(8,128)S(1)} copy-done((f32[16,4,128,128]{3,2,1,0:T(8,128)S(1)}, f32[16,4,128,128]{3,2,1,0:T(8,128)}, u32[]{:S(2)}) %copy-start.2) | copy-done | bytes 4194328
  28.4 3.1 %load.1 = (f32[16,4,64,128]{3,2,1,0:T(8,128)S(1)}, f32[16,4,64,128]{3,2,1,0:T(8,128)S(1)}, f32[16,4,64,128]{3,2,1,0:T(8,128)S(1)}, f32[16,4,64,128]{3,2,1,0:T(8,...) custom-call(f32[16,4,128,128]{3,2,1,0:T(8,128)S(1)} %copy-done, ...), custom_call_target="tpu_custom_call" | custom-call | tf_op jit(solution)/shard_map/load/pallas_call | solution.py:21
  33.3 4.9 %collective-permute-start.11 = (f32[16,64,128]{2,1,0:T(8,128)S(1)}, f32[16,64,128]{2,1,0:T(8,128)S(1)}, u32[]{:S(2)}, u32[]{:S(2)}) collective-permute-start(f32[16,64,128]{2,1,0:T(8,128)S(1)} %get-tuple-element.75), channel_id=1, source_target_pairs={{0,4},{4,8},{8,12},{1,5},{5,9},{9,13},{2,6},{6,10},{10,14},{3,7},{... | collective-permute-start | bytes 1572872 | tf_op jit(solution)/shard_map/ppermute | solution.py:45
  39.5 1.9 %step_mid_1_0_1_2_3.3 = (f32[16,4,64,128]{3,2,1,0:T(8,128)S(1)}, f32[16,64,128]{2,1,0:T(8,128)S(1)}, f32[16,64,128]{2,1,0:T(8,128)S(1)}, f32[4,64,128]{2,1,0:T(8,128)S(1)}, f32[16,4,128]{2,1,0:T(4,128)S(1)}) custom-call(f32[16,4,64,128]{3,2,1,0:T(8,128)S(1)} %get-tuple-element.56.refs_3_.refs_0_, f32[16,4,64,128]{3,2,1,0:T(8,128)S(1)} %get-tuple-element.57.refs_1_, ...), custom_call_target="tpu_custom_call" | custom-call | flops 5242880 | tf_op jit(solution)/shard_map/step_mid_1_0_1_2_3/pallas_call | solution.py:21
  41.4 4.6 %collective-permute-start.7 = (f32[16,64,128]{2,1,0:T(8,128)S(1)}, f32[16,64,128]{2,1,0:T(8,128)S(1)}, u32[]{:S(2)}, u32[]{:S(2)}) collective-permute-start(f32[16,64,128]{2,1,0:T(8,128)S(1)} %get-tuple-element.71), channel_id=1, source_target_pairs={{0,4},{4,8},{8,12},{1,5},{5,9},{9,13},{2,6},{6,10},{10,14},{3,7},{... | collective-permute-start | bytes 1572872 | tf_op jit(solution)/shard_map/ppermute | solution.py:45
  48.8 2.4 %collective-permute-done.10.refs_7_ = f32[16,4,128]{2,1,0:T(4,128)S(1)} collective-permute-done((f32[16,4,128]{2,1,0:T(4,128)S(1)}, f32[16,4,128]{2,1,0:T(4,128)S(1)}, u32[]{:S(2)}, u32[]{:S(2)}) %collective-permute-start.10) | collective-permute-done | bytes 32800 | tf_op jit(solution)/shard_map/ppermute | solution.py:45
  51.8 4.5 %collective-permute-done.13.refs_6_ = f32[4,64,128]{2,1,0:T(8,128)S(1)} collective-permute-done((f32[4,64,128]{2,1,0:T(8,128)S(1)}, f32[4,64,128]{2,1,0:T(8,128)S(1)}, u32[]{:S(2)}, u32[]{:S(2)}) %collective-permute-start.13) | collective-permute-done | bytes 131104 | tf_op jit(solution)/shard_map/ppermute | solution.py:45
  58.6 4.6 %collective-permute-start.18 = (f32[16,64,128]{2,1,0:T(8,128)S(1)}, f32[16,64,128]{2,1,0:T(8,128)S(1)}, u32[]{:S(2)}, u32[]{:S(2)}) collective-permute-start(f32[16,64,128]{2,1,0:T(8,128)S(1)} %get-tuple-element.84), channel_id=1, source_target_pairs={{0,4},{4,8},{8,12},{1,5},{5,9},{9,13},{2,6},{6,10},{10,14},{3,7},{... | collective-permute-start | bytes 1572872 | tf_op jit(solution)/shard_map/ppermute | solution.py:45
  64.5 1.9 %step_mid_1_0_1_2_3.4 = (f32[16,4,64,128]{3,2,1,0:T(8,128)S(1)}, f32[16,64,128]{2,1,0:T(8,128)S(1)}, f32[16,64,128]{2,1,0:T(8,128)S(1)}, f32[4,64,128]{2,1,0:T(8,128)S(1)}, f32[16,4,128]{2,1,0:T(4,128)S(1)}) custom-call(f32[16,4,64,128]{3,2,1,0:T(8,128)S(1)} %get-tuple-element.70.refs_3_.refs_0_, f32[16,4,64,128]{3,2,1,0:T(8,128)S(1)} %get-tuple-element.57.refs_1_, ...), custom_call_target="tpu_custom_call" | custom-call | flops 5242880 | tf_op jit(solution)/shard_map/step_mid_1_0_1_2_3/pallas_call | solution.py:21
  66.4 4.6 %collective-permute-start.14 = (f32[16,64,128]{2,1,0:T(8,128)S(1)}, f32[16,64,128]{2,1,0:T(8,128)S(1)}, u32[]{:S(2)}, u32[]{:S(2)}) collective-permute-start(f32[16,64,128]{2,1,0:T(8,128)S(1)} %get-tuple-element.80), channel_id=1, source_target_pairs={{0,4},{4,8},{8,12},{1,5},{5,9},{9,13},{2,6},{6,10},{10,14},{3,7},{... | collective-permute-start | bytes 1572872 | tf_op jit(solution)/shard_map/ppermute | solution.py:45
  73.8 2.4 %collective-permute-done.17.refs_7_ = f32[16,4,128]{2,1,0:T(4,128)S(1)} collective-permute-done((f32[16,4,128]{2,1,0:T(4,128)S(1)}, f32[16,4,128]{2,1,0:T(4,128)S(1)}, u32[]{:S(2)}, u32[]{:S(2)}) %collective-permute-start.17) | collective-permute-done | bytes 32800 | tf_op jit(solution)/shard_map/ppermute | solution.py:45
  77.8 3.4 %collective-permute-done.20.refs_6_ = f32[4,64,128]{2,1,0:T(8,128)S(1)} collective-permute-done((f32[4,64,128]{2,1,0:T(8,128)S(1)}, f32[4,64,128]{2,1,0:T(8,128)S(1)}, u32[]{:S(2)}, u32[]{:S(2)}) %collective-permute-start.20) | collective-permute-done | bytes 131104 | tf_op jit(solution)/shard_map/ppermute | solution.py:45
  84.6 4.6 %collective-permute-start.26 = (f32[16,64,128]{2,1,0:T(8,128)S(1)}, f32[16,64,128]{2,1,0:T(8,128)S(1)}, u32[]{:S(2)}, u32[]{:S(2)}) collective-permute-start(f32[16,64,128]{2,1,0:T(8,128)S(1)} %get-tuple-element.95), channel_id=1, source_target_pairs={{0,4},{4,8},{8,12},{1,5},{5,9},{9,13},{2,6},{6,10},{10,14},{3,7},{... | collective-permute-start | bytes 1572872 | tf_op jit(solution)/shard_map/ppermute | solution.py:45
  92.4 4.6 %collective-permute-start.21 = (f32[16,64,128]{2,1,0:T(8,128)S(1)}, f32[16,64,128]{2,1,0:T(8,128)S(1)}, u32[]{:S(2)}, u32[]{:S(2)}) collective-permute-start(f32[16,64,128]{2,1,0:T(8,128)S(1)} %get-tuple-element.89), channel_id=1, source_target_pairs={{0,4},{4,8},{8,12},{1,5},{5,9},{9,13},{2,6},{6,10},{10,14},{3,7},{... | collective-permute-start | bytes 1572872 | tf_op jit(solution)/shard_map/ppermute | solution.py:45
  99.8 2.4 %collective-permute-done.24.refs_7_.refs_5_ = f32[16,4,128]{2,1,0:T(4,128)S(1)} collective-permute-done((f32[16,4,128]{2,1,0:T(4,128)S(1)}, f32[16,4,128]{2,1,0:T(4,128)S(1)}, u32[]{:S(2)}, u32[]{:S(2)}) %collective-permute-start.24) | collective-permute-done | bytes 32800 | tf_op jit(solution)/shard_map/ppermute | solution.py:45
  102.7 5.9 %collective-permute-done.28.refs_6_.refs_4_ = f32[4,64,128]{2,1,0:T(8,128)S(1)} collective-permute-done((f32[4,64,128]{2,1,0:T(8,128)S(1)}, f32[4,64,128]{2,1,0:T(8,128)S(1)}, u32[]{:S(2)}, u32[]{:S(2)}) %collective-permute-start.28) | collective-permute-done | bytes 131104 | tf_op jit(solution)/shard_map/ppermute | solution.py:45
  109.7 3.9 %collective-permute-done.23.refs_6_.refs_4_ = f32[4,64,128]{2,1,0:T(8,128)S(1)} collective-permute-done((f32[4,64,128]{2,1,0:T(8,128)S(1)}, f32[4,64,128]{2,1,0:T(8,128)S(1)}, u32[]{:S(2)}, u32[]{:S(2)}) %collective-permute-start.23) | collective-permute-done | bytes 131104 | tf_op jit(solution)/shard_map/ppermute | solution.py:45
  114.7 2.1 %collective-permute-start.30 = (f32[2,2,64,128]{3,2,1,0:T(8,128)S(1)}, f32[2,2,64,128]{3,2,1,0:T(8,128)S(1)}, u32[]{:S(2)}, u32[]{:S(2)}) collective-permute-start(f32[2,2,64,128]{3,2,1,0:T(8,128)S(1)} %get-tuple-element.101.refs_1_), channel_id=1, source_target_pairs={{0,16},{16,0},{1,17},{17,1},{2,18},{18,2},{3,19},{19,3},{4,20},{20... | collective-permute-start | bytes 393224 | tf_op jit(solution)/shard_map/ppermute | solution.py:337
  119.3 2.1 %collective-permute-start.25 = (f32[2,2,64,128]{3,2,1,0:T(8,128)S(1)}, f32[2,2,64,128]{3,2,1,0:T(8,128)S(1)}, u32[]{:S(2)}, u32[]{:S(2)}) collective-permute-start(f32[2,2,64,128]{3,2,1,0:T(8,128)S(1)} %get-tuple-element.94.refs_1_), channel_id=1, source_target_pairs={{0,16},{16,0},{1,17},{17,1},{2,18},{18,2},{3,19},{19,3},{4,20},{20... | collective-permute-start | bytes 393224 | tf_op jit(solution)/shard_map/ppermute | solution.py:337
  (62 shorter events, 41.9 us)
Async XLA Ops:
  3.2 28.3 %collective-permute-start.4 = (f32[16,64,128]{2,1,0:T(8,128)S(1)}, f32[16,64,128]{2,1,0:T(8,128)S(1)}, u32[]{:S(2)}, u32[]{:S(2)}) collective-permute-start(f32[16,64,128]{2,1,0:T(8,128)S(1)} %get-tuple-element.66), channel_id=1, source_target_pairs={{0,4},{4,8},{8,12},{1,5},{5,9},{9,13},{2,6},{6,10},{10,14},{3,7},{... | collective-permute-start | bytes 1572872 | tf_op jit(solution)/shard_map/ppermute | solution.py:45
  8.4 23.1 %collective-permute-start.5 = (f32[16,64,128]{2,1,0:T(8,128)S(1)}, f32[16,64,128]{2,1,0:T(8,128)S(1)}, u32[]{:S(2)}, u32[]{:S(2)}) collective-permute-start(f32[16,64,128]{2,1,0:T(8,128)S(1)} %get-tuple-element.67), channel_id=1, source_target_pairs={{4,0},{8,4},{12,8},{5,1},{9,5},{13,9},{6,2},{10,6},{14,10},{7,3},{... | collective-permute-start | bytes 1572872 | tf_op jit(solution)/shard_map/ppermute | solution.py:45
  9.7 29.8 %collective-permute-start = (f32[16,64,128]{2,1,0:T(8,128)S(1)}, f32[16,64,128]{2,1,0:T(8,128)S(1)}, u32[]{:S(2)}, u32[]{:S(2)}) collective-permute-start(f32[16,64,128]{2,1,0:T(8,128)S(1)} %get-tuple-element.60), channel_id=1, source_target_pairs={{0,4},{4,8},{8,12},{1,5},{5,9},{9,13},{2,6},{6,10},{10,14},{3,7},{... | collective-permute-start | bytes 1572872 | tf_op jit(solution)/shard_map/ppermute | solution.py:45
  14.3 25.2 %collective-permute-start.1 = (f32[16,64,128]{2,1,0:T(8,128)S(1)}, f32[16,64,128]{2,1,0:T(8,128)S(1)}, u32[]{:S(2)}, u32[]{:S(2)}) collective-permute-start(f32[16,64,128]{2,1,0:T(8,128)S(1)} %get-tuple-element.61), channel_id=1, source_target_pairs={{4,0},{8,4},{12,8},{5,1},{9,5},{13,9},{6,2},{10,6},{14,10},{7,3},{... | collective-permute-start | bytes 1572872 | tf_op jit(solution)/shard_map/ppermute | solution.py:45
  24.7 14.8 %collective-permute-start.2 = (f32[4,64,128]{2,1,0:T(8,128)S(1)}, f32[4,64,128]{2,1,0:T(8,128)S(1)}, u32[]{:S(2)}, u32[]{:S(2)}) collective-permute-start(f32[4,64,128]{2,1,0:T(8,128)S(1)} %get-tuple-element.62), channel_id=1, source_target_pairs={{0,16},{16,0},{1,17},{17,1},{2,18},{18,2},{3,19},{19,3},{4,20},{20... | collective-permute-start | bytes 393224 | tf_op jit(solution)/shard_map/ppermute | solution.py:45
  33.3 23.4 %collective-permute-start.11 = (f32[16,64,128]{2,1,0:T(8,128)S(1)}, f32[16,64,128]{2,1,0:T(8,128)S(1)}, u32[]{:S(2)}, u32[]{:S(2)}) collective-permute-start(f32[16,64,128]{2,1,0:T(8,128)S(1)} %get-tuple-element.75), channel_id=1, source_target_pairs={{0,4},{4,8},{8,12},{1,5},{5,9},{9,13},{2,6},{6,10},{10,14},{3,7},{... | collective-permute-start | bytes 1572872 | tf_op jit(solution)/shard_map/ppermute | solution.py:45
  38.2 18.6 %collective-permute-start.12 = (f32[16,64,128]{2,1,0:T(8,128)S(1)}, f32[16,64,128]{2,1,0:T(8,128)S(1)}, u32[]{:S(2)}, u32[]{:S(2)}) collective-permute-start(f32[16,64,128]{2,1,0:T(8,128)S(1)} %get-tuple-element.76), channel_id=1, source_target_pairs={{4,0},{8,4},{12,8},{5,1},{9,5},{13,9},{6,2},{10,6},{14,10},{7,3},{... | collective-permute-start | bytes 1572872 | tf_op jit(solution)/shard_map/ppermute | solution.py:45
  41.4 23.1 %collective-permute-start.7 = (f32[16,64,128]{2,1,0:T(8,128)S(1)}, f32[16,64,128]{2,1,0:T(8,128)S(1)}, u32[]{:S(2)}, u32[]{:S(2)}) collective-permute-start(f32[16,64,128]{2,1,0:T(8,128)S(1)} %get-tuple-element.71), channel_id=1, source_target_pairs={{0,4},{4,8},{8,12},{1,5},{5,9},{9,13},{2,6},{6,10},{10,14},{3,7},{... | collective-permute-start | bytes 1572872 | tf_op jit(solution)/shard_map/ppermute | solution.py:45
  46.0 18.5 %collective-permute-start.8 = (f32[16,64,128]{2,1,0:T(8,128)S(1)}, f32[16,64,128]{2,1,0:T(8,128)S(1)}, u32[]{:S(2)}, u32[]{:S(2)}) collective-permute-start(f32[16,64,128]{2,1,0:T(8,128)S(1)} %get-tuple-element.72), channel_id=1, source_target_pairs={{4,0},{8,4},{12,8},{5,1},{9,5},{13,9},{6,2},{10,6},{14,10},{7,3},{... | collective-permute-start | bytes 1572872 | tf_op jit(solution)/shard_map/ppermute | solution.py:45
  56.2 8.2 %collective-permute-start.9 = (f32[4,64,128]{2,1,0:T(8,128)S(1)}, f32[4,64,128]{2,1,0:T(8,128)S(1)}, u32[]{:S(2)}, u32[]{:S(2)}) collective-permute-start(f32[4,64,128]{2,1,0:T(8,128)S(1)} %get-tuple-element.73), channel_id=1, source_target_pairs={{0,16},{16,0},{1,17},{17,1},{2,18},{18,2},{3,19},{19,3},{4,20},{20... | collective-permute-start | bytes 393224 | tf_op jit(solution)/shard_map/ppermute | solution.py:45
  58.6 24.2 %collective-permute-start.18 = (f32[16,64,128]{2,1,0:T(8,128)S(1)}, f32[16,64,128]{2,1,0:T(8,128)S(1)}, u32[]{:S(2)}, u32[]{:S(2)}) collective-permute-start(f32[16,64,128]{2,1,0:T(8,128)S(1)} %get-tuple-element.84), channel_id=1, source_target_pairs={{0,4},{4,8},{8,12},{1,5},{5,9},{9,13},{2,6},{6,10},{10,14},{3,7},{... | collective-permute-start | bytes 1572872 | tf_op jit(solution)/shard_map/ppermute | solution.py:45
  63.2 19.6 %collective-permute-start.19 = (f32[16,64,128]{2,1,0:T(8,128)S(1)}, f32[16,64,128]{2,1,0:T(8,128)S(1)}, u32[]{:S(2)}, u32[]{:S(2)}) collective-permute-start(f32[16,64,128]{2,1,0:T(8,128)S(1)} %get-tuple-element.85), channel_id=1, source_target_pairs={{4,0},{8,4},{12,8},{5,1},{9,5},{13,9},{6,2},{10,6},{14,10},{7,3},{... | collective-permute-start | bytes 1572872 | tf_op jit(solution)/shard_map/ppermute | solution.py:45
  66.4 24.1 %collective-permute-start.14 = (f32[16,64,128]{2,1,0:T(8,128)S(1)}, f32[16,64,128]{2,1,0:T(8,128)S(1)}, u32[]{:S(2)}, u32[]{:S(2)}) collective-permute-start(f32[16,64,128]{2,1,0:T(8,128)S(1)} %get-tuple-element.80), channel_id=1, source_target_pairs={{0,4},{4,8},{8,12},{1,5},{5,9},{9,13},{2,6},{6,10},{10,14},{3,7},{... | collective-permute-start | bytes 1572872 | tf_op jit(solution)/shard_map/ppermute | solution.py:45
  71.0 19.5 %collective-permute-start.15 = (f32[16,64,128]{2,1,0:T(8,128)S(1)}, f32[16,64,128]{2,1,0:T(8,128)S(1)}, u32[]{:S(2)}, u32[]{:S(2)}) collective-permute-start(f32[16,64,128]{2,1,0:T(8,128)S(1)} %get-tuple-element.81), channel_id=1, source_target_pairs={{4,0},{8,4},{12,8},{5,1},{9,5},{13,9},{6,2},{10,6},{14,10},{7,3},{... | collective-permute-start | bytes 1572872 | tf_op jit(solution)/shard_map/ppermute | solution.py:45
  81.2 9.2 %collective-permute-start.16 = (f32[4,64,128]{2,1,0:T(8,128)S(1)}, f32[4,64,128]{2,1,0:T(8,128)S(1)}, u32[]{:S(2)}, u32[]{:S(2)}) collective-permute-start(f32[4,64,128]{2,1,0:T(8,128)S(1)} %get-tuple-element.82), channel_id=1, source_target_pairs={{0,16},{16,0},{1,17},{17,1},{2,18},{18,2},{3,19},{19,3},{4,20},{20... | collective-permute-start | bytes 393224 | tf_op jit(solution)/shard_map/ppermute | solution.py:45
  84.6 30.1 %collective-permute-start.26 = (f32[16,64,128]{2,1,0:T(8,128)S(1)}, f32[16,64,128]{2,1,0:T(8,128)S(1)}, u32[]{:S(2)}, u32[]{:S(2)}) collective-permute-start(f32[16,64,128]{2,1,0:T(8,128)S(1)} %get-tuple-element.95), channel_id=1, source_target_pairs={{0,4},{4,8},{8,12},{1,5},{5,9},{9,13},{2,6},{6,10},{10,14},{3,7},{... | collective-permute-start | bytes 1572872 | tf_op jit(solution)/shard_map/ppermute | solution.py:45
  89.1 27.6 %collective-permute-start.27 = (f32[16,64,128]{2,1,0:T(8,128)S(1)}, f32[16,64,128]{2,1,0:T(8,128)S(1)}, u32[]{:S(2)}, u32[]{:S(2)}) collective-permute-start(f32[16,64,128]{2,1,0:T(8,128)S(1)} %get-tuple-element.96), channel_id=1, source_target_pairs={{4,0},{8,4},{12,8},{5,1},{9,5},{13,9},{6,2},{10,6},{14,10},{7,3},{... | collective-permute-start | bytes 1572872 | tf_op jit(solution)/shard_map/ppermute | solution.py:45
  92.4 25.7 %collective-permute-start.21 = (f32[16,64,128]{2,1,0:T(8,128)S(1)}, f32[16,64,128]{2,1,0:T(8,128)S(1)}, u32[]{:S(2)}, u32[]{:S(2)}) collective-permute-start(f32[16,64,128]{2,1,0:T(8,128)S(1)} %get-tuple-element.89), channel_id=1, source_target_pairs={{0,4},{4,8},{8,12},{1,5},{5,9},{9,13},{2,6},{6,10},{10,14},{3,7},{... | collective-permute-start | bytes 1572872 | tf_op jit(solution)/shard_map/ppermute | solution.py:45
  96.9 21.1 %collective-permute-start.22 = (f32[16,64,128]{2,1,0:T(8,128)S(1)}, f32[16,64,128]{2,1,0:T(8,128)S(1)}, u32[]{:S(2)}, u32[]{:S(2)}) collective-permute-start(f32[16,64,128]{2,1,0:T(8,128)S(1)} %get-tuple-element.90), channel_id=1, source_target_pairs={{4,0},{8,4},{12,8},{5,1},{9,5},{13,9},{6,2},{10,6},{14,10},{7,3},{... | collective-permute-start | bytes 1572872 | tf_op jit(solution)/shard_map/ppermute | solution.py:45
  102.2 6.4 %collective-permute-start.28 = (f32[4,64,128]{2,1,0:T(8,128)S(1)}, f32[4,64,128]{2,1,0:T(8,128)S(1)}, u32[]{:S(2)}, u32[]{:S(2)}) collective-permute-start(f32[4,64,128]{2,1,0:T(8,128)S(1)} %get-tuple-element.97), channel_id=1, source_target_pairs={{0,16},{16,0},{1,17},{17,1},{2,18},{18,2},{3,19},{19,3},{4,20},{20... | collective-permute-start | bytes 393224 | tf_op jit(solution)/shard_map/ppermute | solution.py:45
  113.6 7.8 %collective-permute-start.31 = (f32[2,2,64,128]{3,2,1,0:T(8,128)S(1)}, f32[2,2,64,128]{3,2,1,0:T(8,128)S(1)}, u32[]{:S(2)}, u32[]{:S(2)}) collective-permute-start(f32[2,2,64,128]{3,2,1,0:T(8,128)S(1)} %get-tuple-element.103.refs_1_), channel_id=1, source_target_pairs={{0,16},{16,0},{1,17},{17,1},{2,18},{18,2},{3,19},{19,3},{4,20},{20... | collective-permute-start | bytes 393224 | tf_op jit(solution)/shard_map/ppermute | solution.py:337
  114.7 8.0 %collective-permute-start.30 = (f32[2,2,64,128]{3,2,1,0:T(8,128)S(1)}, f32[2,2,64,128]{3,2,1,0:T(8,128)S(1)}, u32[]{:S(2)}, u32[]{:S(2)}) collective-permute-start(f32[2,2,64,128]{3,2,1,0:T(8,128)S(1)} %get-tuple-element.101.refs_1_), channel_id=1, source_target_pairs={{0,16},{16,0},{1,17},{17,1},{2,18},{18,2},{3,19},{19,3},{4,20},{20... | collective-permute-start | bytes 393224 | tf_op jit(solution)/shard_map/ppermute | solution.py:337
  118.0 6.1 %collective-permute-start.29 = (f32[2,2,64,128]{3,2,1,0:T(8,128)S(1)}, f32[2,2,64,128]{3,2,1,0:T(8,128)S(1)}, u32[]{:S(2)}, u32[]{:S(2)}) collective-permute-start(f32[2,2,64,128]{3,2,1,0:T(8,128)S(1)} %get-tuple-element.99.refs_1_), channel_id=1, source_target_pairs={{0,16},{16,0},{1,17},{17,1},{2,18},{18,2},{3,19},{19,3},{4,20},{20... | collective-permute-start | bytes 393224 | tf_op jit(solution)/shard_map/ppermute | solution.py:337
  119.3 6.2 %collective-permute-start.25 = (f32[2,2,64,128]{3,2,1,0:T(8,128)S(1)}, f32[2,2,64,128]{3,2,1,0:T(8,128)S(1)}, u32[]{:S(2)}, u32[]{:S(2)}) collective-permute-start(f32[2,2,64,128]{3,2,1,0:T(8,128)S(1)} %get-tuple-element.94.refs_1_), channel_id=1, source_target_pairs={{0,16},{16,0},{1,17},{17,1},{2,18},{18,2},{3,19},{19,3},{4,20},{20... | collective-permute-start | bytes 393224 | tf_op jit(solution)/shard_map/ppermute | solution.py:337
  (11 other events, 63.7 us)
